TPU v7x, 32 devices: a whole 2x2x4 slice. The times are simulated.
32 devices in a mesh: grp: 2 (over y), seq: 16 (over z, x, core), head: 1.
Axes of the slice: x: 2, y: 2, z: 4, core: 2. Of those that a mesh axis runs over, the one named last changes fastest.
Arguments:
- queries: bfloat16 [2048, 1, 128], P(('grp', 'seq'), 'head'), parts along dimension 0, may hold values from -6 to 6
- keys: bfloat16 [256, 512, 8, 128], P(('grp', 'seq'), None, 'head'), parts along dimension 0, may hold values from -28 to 28
- values: bfloat16 [256, 512, 8, 128], P(('grp', 'seq'), None, 'head'), parts along dimension 0, may hold values from -6 to 6
- lengths: int32 [32], P('grp'), parts along dimension 0, may hold values from 1 to 4096, 40960 in all
- slot_block: int32 [256], P(('grp', 'seq')), parts along dimension 0, may hold values from 0 to 127, each once
Outputs:
- attended: bfloat16 [2048, 1, 128], P(('grp', 'seq'), 'head'), parts along dimension 0
There are 2 independent parts, one for each index of `grp`. A program takes and returns all parts, laid end to end along the dimension named above; each array names one. Nothing has to cross between parts.
Inputs may be any that keep to these rules, and one draw needn't show every extreme that they name: `slot_block`: each slot holds a different logical block; every block of every sequence has a slot. `lengths`: every sequence has at least one token.
All inputs are finite; a program needn't handle non-finite values.
Results may differ from a plain program's by a relative error of at most 0.0055.
Values may be sent and summed in bfloat16 or wider, within the bound.
A program may use at most 64 MiB of HBM per device.

v0:
```python
import jax
import jax.numpy as jnp
from jax import lax
from jax.sharding import PartitionSpec as P


def slot_partial(q_one, key_one, val_one, live_one, factor):
    scores = jnp.einsum("kgd,tkd->kgt", q_one, key_one, preferred_element_type=jnp.float32) * factor
    live_row = live_one[None, None, :]
    peak = jnp.max(jnp.where(live_row, scores, -1e30), axis=-1)
    weights = jnp.where(live_row, jnp.exp(scores - peak[..., None]), 0.0).astype(jnp.bfloat16)
    total = jnp.sum(weights.astype(jnp.float32), axis=-1)
    partial_out = jnp.einsum("kgt,tkd->kgd", weights, val_one, preferred_element_type=jnp.float32)
    return (peak, total, partial_out)


def body(queries, keys, values, lengths, slot_block):
    rows = lax.all_gather(queries, "seq", axis=0, tiled=True)
    slots, block, kv_local, head_dim = keys.shape
    batch = lengths.shape[0]
    group = rows.shape[0] // batch // kv_local
    factor = head_dim ** (-0.5)
    q_grouped = rows.reshape(batch, kv_local, group, head_dim)
    per_seq = slots * lax.axis_size("seq") // batch
    seq_of = slot_block // per_seq
    blk_of = slot_block % per_seq
    q_slot = jnp.take(q_grouped, seq_of, axis=0)
    positions = blk_of[:, None] * block + jnp.arange(block, dtype=jnp.int32)[None, :]
    live = positions < jnp.take(lengths, seq_of)[:, None]

    def run_slot(q_one, key_one, val_one, live_one):
        return slot_partial(q_one, key_one, val_one, live_one, factor)

    peaks, totals, partials = jax.vmap(run_slot)(q_slot, keys, values, live)
    member = seq_of[:, None] == jnp.arange(batch, dtype=jnp.int32)[None, :]
    best = jnp.max(jnp.where(member[:, :, None, None], peaks[:, None], -1e30), axis=0)
    scaled = jnp.exp(peaks - jnp.take(best, seq_of, axis=0))
    onehot = member.astype(jnp.float32)
    denom = jnp.einsum("sb,skg->bkg", onehot, scaled * totals, precision=lax.Precision.HIGHEST)
    numer = jnp.einsum(
        "sb,skgd->bkgd", onehot, scaled[..., None] * partials, precision=lax.Precision.HIGHEST
    )
    row_count = rows.shape[0]
    share = row_count // lax.axis_size("seq")
    top_peak = lax.pmax(best, "seq")
    rescale = jnp.exp(best - top_peak)
    own_total, own_out = (
        lax.psum_scatter(
            (denom * rescale).reshape(row_count), "seq", scatter_dimension=0, tiled=True
        ),
        lax.psum_scatter(
            (numer * rescale[..., None]).reshape(row_count, head_dim),
            "seq",
            scatter_dimension=0,
            tiled=True,
        ),
    )
    result = own_out / own_total[:, None]
    return result.astype(jnp.bfloat16).reshape(share, 1, head_dim)


def solution(mesh):
    placed = (
        P(("grp", "seq"), "head", None),
        P(("grp", "seq"), None, "head", None),
        P(("grp", "seq"), None, "head", None),
        P("grp"),
        P(("grp", "seq")),
    )
    return jax.shard_map(
        body, mesh=mesh, in_specs=placed, out_specs=P(("grp", "seq"), "head", None), check_vma=False
    )
```

profile of v0, /device:TPU:0, one launch (start us, length us, event | category | flops | bytes accessed | tf_op | source)
XLA Modules:
  0.0 166.0 jit_solution(9803594081013029989)
XLA Ops:
  6.5 0.7 compare_select_fusion
  7.3 0.6 gather_fusion
  8.0 24.1 %all_gather.3 = bf16[1024,1,128]{2,0,1:T(8,128)(2,1)S(1)} all-gather(bf16[64,1,128]{2,0,1:T(8,128)(2,1)} %param.5), channel_id=1, replica_groups=mesh['grp'=2,'seq'=16,'head'=1] {'seq'}, dimensions={0}, use_global_device_ids=true | all-gather | bytes 278528 | tf_op jit(solution)/shard_map/all_gather | solution.py:18
  32.0 0.6 gather_fusion.1
  32.6 0.1 add_compare_fusion
  32.7 5.8 %select_reduce_fusion = (f32[8,8,8]{2,1,0:T(8,128)S(1)}, f32[8,8,8,512]{3,2,1,0:T(8,128)S(1)}) fusion(pred[8,512]{1,0:T(8,128)(4,1)S(1)} %add_compare_fusion, bf16[8,512,8,128]{3,2,1,0:T(8,128)(2,1)} %param.6, bf16[8,8,8,128]{3,2,1,0:T(8,128)(2,1)S(1)} %gather_fusion.1, pred[8]{0:T(512)(128)(4,1)S(1)} %get-tuple-element.8), kind=kOutput, calls=%fused_computation.14 | convolution fusion | flops 67960320 | bytes 9574408 | tf_op jit(solution)/shard_map/vmap(kgd,tkd->kgt)/dot_general | solution.py:8
  38.4 0.1 select_reduce_fusion.1
  38.6 57.8 %pmax.7 = f32[16,8,8]{0,2,1:T(8,128)S(1)} all-reduce(f32[16,8,8]{0,2,1:T(8,128)S(1)} %select_reduce_fusion.1), channel_id=1, replica_groups=mesh['grp'=2,'seq'=16,'head'=1] {'seq'}, use_global_device_ids=true, to_apply=%region_2.3 | all-reduce | flops 1024 | bytes 8192 | tf_op jit(solution)/shard_map/pmax | solution.py:45
  96.4 0.1 copy.23
  96.6 0.3 convert_reduce_fusion
  96.9 0.6 gather_fusion.2
  97.5 0.1 fusion.23
  97.6 5.0 %fusion.7 = f32[8,8,8,128]{3,2,1,0:T(8,128)S(1)} fusion(bf16[8,512,8,128]{3,2,1,0:T(8,128)(2,1)} %param.7, f32[8,8,8]{2,1,0:T(8,128)S(1)} %get-tuple-element.6, f32[8,8,8,512]{3,2,1,0:T(8,128)S(1)} %get-tuple-element.13, f32[8,8,8]{2,1,0:T(8,128)S(1)} %get-tuple-element.12, pred[8,512]{1,0:T(8,128)(4,1)S(1)} %add_compare_fusion), kind=kOutput, calls=%fused_computation.9 | convolution fusion | flops 67960832 | bytes 9707520 | tf_op jit(solution)/shard_map/vmap(kgt,tkd->kgd)/dot_general | solution.py:13
  102.5 0.6 convolution_multiply_fusion
  103.1 1.0 copy.26
  104.1 0.1 copy.27
  104.2 0.2 fusion.10
  104.4 0.1 copy.28
  104.5 0.1 reshape.84
  104.6 0.6 dynamic-slice
  105.8 29.6 %all-reduce = f32[1024]{0:T(1024)S(1)} all-reduce(f32[1024]{0:T(1024)S(1)} %reshape.84), channel_id=3, replica_groups=mesh['grp'=2,'seq'=16,'head'=1] {'seq'}, use_global_device_ids=true, to_apply=%region_5.6.clone | all-reduce | flops 1024 | bytes 8192
  135.4 0.1 dynamic-slice.1
  135.5 22.2 %reduce-scatter.2.cloned.1.call-done = f32[64,128]{1,0:T(8,128)} async-done(((f32[1024,128]{1,0:T(8,128)}), f32[64,128]{1,0:T(8,128)}) %reduce-scatter.2.cloned.1.call-update) | async-done | bytes 32784 | tf_op jit(solution)/shard_map/reduce_scatter | solution.py:51
  157.7 1.4 fusion.16
  (10 shorter events, 0.1 us)
Async XLA Ops:
  6.5 0.8 copy-start
  6.5 151.2 %reduce-scatter.2.cloned.1.call-start = ((), (), s32[]{:S(2)}) async-start(), calls=%async_computation.1 | async-start | bytes 557056 | tf_op jit(solution)/shard_map/reduce_scatter | solution.py:51
  38.4 66.1 %copy-start.1 = (u32[32]{0:T(128)S(1)}, u32[32]{0:T(128)}, u32[]{:S(2)}) copy-start(u32[32]{0:T(128)} %constant.84) | copy-start | bytes 388
Sparse Core Ops, SparseCore 0:
  104.2 53.4 reduce-scatter.1
where the time goes:
time: 166 us
  blocking collectives  111 us (67%)
  waiting for transfers between devices  22.2 us (13%)
  between operations  14.1 us (8%)
  matrix products  11.5 us (7%)
  local copies, waits for them, and re-layouts  3.73 us (2%)
  other arithmetic  2.89 us (2%)
    pmax x1, blocking collectives, body(): top_peak = lax.pmax(best, 'seq')  57.8 us
    unnamed x1, blocking collectives  29.6 us
    all_gather x1, blocking collectives, body(): rows = lax.all_gather(queries, 'seq', axis=0, tiled=True)  24.1 us
    reduce_scatter x1, waiting for transfers between devices, body(): lax.psum_scatter((numer * rescale[..., None]).reshape(row_count, head_dim...  22.2 us
    dot_general x1, matrix products, slot_partial(): jnp.einsum('kgd,tkd->kgt', q_one, key_one, preferred_element_type=jnp.flo...  5.79 us
    dot_general x1, matrix products, slot_partial(): jnp.einsum('kgt,tkd->kgd', weights, val_one, preferred_element_type=jnp.f...  4.96 us
  transfers between devices with their start and end apart: 1, of which 1 were waited for; matrix products, arithmetic and copies ran while one was open for 1% of the time, Pallas kernels for 0%

commit v1 on v0

--- a/solution.py
+++ b/solution.py
@@ -15,7 +15,12 @@
 
 
 def body(queries, keys, values, lengths, slot_block):
-    rows = lax.all_gather(queries, "seq", axis=0, tiled=True)
+    ring = [queries]
+    for hop in range(15):
+        ring.append(lax.ppermute(ring[-1], "seq", [(dev, (dev + 1) % 16) for dev in range(16)]))
+    rows = jnp.roll(
+        jnp.concatenate(ring[::-1], axis=0), (lax.axis_index("seq") + 1) * ring[0].shape[0], axis=0
+    )
     slots, block, kv_local, head_dim = keys.shape
     batch = lengths.shape[0]
     group = rows.shape[0] // batch // kv_local

time: 166 us -> 232 us (1.40)
  waiting for transfers between devices: 22.2 us -> 110 us
  blocking collectives: 111 us -> 87.2 us
    ppermute x0 -> x15, waiting for transfers between devices: none -> 87.1 us  [body(): lax.ppermute(ring[-1], 'seq', [(dev, (dev + 1) % 16) for dev in range(16)])]
    all_gather x1 -> x0, blocking collectives: 24.1 us -> none  [body(): rows = lax.all_gather(queries, 'seq', axis=0, tiled=True)]
  transfers between devices with their start and end apart: 1 -> 16, of which waited for: 1 -> 16; matrix products, arithmetic and copies ran while one was open for 1% -> 1% of each run, Pallas kernels for 0% -> 0%
where the time goes in v1:
time: 232 us
  waiting for transfers between devices  110 us (47%)
  blocking collectives  87.2 us (38%)
  between operations  14.3 us (6%)
  matrix products  11.5 us (5%)
  local copies, waits for them, and re-layouts  5.47 us (2%)
  other arithmetic  2.87 us (1%)
    ppermute x15, waiting for transfers between devices, body(): lax.ppermute(ring[-1], 'seq', [(dev, (dev + 1) % 16) for dev in range(16)])  87.1 us
    pmax x1, blocking collectives, body(): top_peak = lax.pmax(best, 'seq')  57.6 us
    unnamed x1, blocking collectives  29.6 us
    reduce_scatter x1, waiting for transfers between devices, body(): lax.psum_scatter((numer * rescale[..., None]).reshape(row_count, head_dim...  22.7 us
    dot_general x1, matrix products, slot_partial(): jnp.einsum('kgd,tkd->kgt', q_one, key_one, preferred_element_type=jnp.flo...  5.79 us
    dot_general x1, matrix products, slot_partial(): jnp.einsum('kgt,tkd->kgd', weights, val_one, preferred_element_type=jnp.f...  4.97 us
  transfers between devices with their start and end apart: 16, of which 16 were waited for; matrix products, arithmetic and copies ran while one was open for 1% of the time, Pallas kernels for 0%

profile of v1, /device:TPU:0, one launch (start us, length us, event | category | flops | bytes accessed | tf_op | source)
XLA Modules:
  0.0 231.7 jit_solution(11302746372268074752)
XLA Ops:
  7.0 6.6 %collective-permute-done = bf16[64,1,128]{2,0,1:T(8,128)(2,1)S(1)} collective-permute-done((bf16[64,1,128]{2,0,1:T(8,128)(2,1)}, bf16[64,1,128]{2,0,1:T(8,128)(2,1)S(1)}, u32[]{:S(2)}, u32[]{:S(2)}) %collective-permute-start) | collective-permute-done | bytes 16416 | tf_op jit(solution)/shard_map/ppermute | solution.py:20
  13.6 5.9 %collective-permute-done.1 = bf16[64,1,128]{2,0,1:T(8,128)(2,1)S(1)} collective-permute-done((bf16[64,1,128]{2,0,1:T(8,128)(2,1)S(1)}, bf16[64,1,128]{2,0,1:T(8,128)(2,1)S(1)}, u32[]{:S(2)}, u32[]{:S(2)}) %collective-permute-start.1) | collective-permute-done | bytes 16416 | tf_op jit(solution)/shard_map/ppermute | solution.py:20
  19.5 5.9 %collective-permute-done.2 = bf16[64,1,128]{2,0,1:T(8,128)(2,1)S(1)} collective-permute-done((bf16[64,1,128]{2,0,1:T(8,128)(2,1)S(1)}, bf16[64,1,128]{2,0,1:T(8,128)(2,1)S(1)}, u32[]{:S(2)}, u32[]{:S(2)}) %collective-permute-start.2) | collective-permute-done | bytes 16416 | tf_op jit(solution)/shard_map/ppermute | solution.py:20
  25.3 5.9 %collective-permute-done.3 = bf16[64,1,128]{2,0,1:T(8,128)(2,1)S(1)} collective-permute-done((bf16[64,1,128]{2,0,1:T(8,128)(2,1)S(1)}, bf16[64,1,128]{2,0,1:T(8,128)(2,1)S(1)}, u32[]{:S(2)}, u32[]{:S(2)}) %collective-permute-start.3) | collective-permute-done | bytes 16416 | tf_op jit(solution)/shard_map/ppermute | solution.py:20
  31.2 5.9 %collective-permute-done.4 = bf16[64,1,128]{2,0,1:T(8,128)(2,1)S(1)} collective-permute-done((bf16[64,1,128]{2,0,1:T(8,128)(2,1)S(1)}, bf16[64,1,128]{2,0,1:T(8,128)(2,1)S(1)}, u32[]{:S(2)}, u32[]{:S(2)}) %collective-permute-start.4) | collective-permute-done | bytes 16416 | tf_op jit(solution)/shard_map/ppermute | solution.py:20
  37.1 5.9 %collective-permute-done.5 = bf16[64,1,128]{2,0,1:T(8,128)(2,1)S(1)} collective-permute-done((bf16[64,1,128]{2,0,1:T(8,128)(2,1)S(1)}, bf16[64,1,128]{2,0,1:T(8,128)(2,1)S(1)}, u32[]{:S(2)}, u32[]{:S(2)}) %collective-permute-start.5) | collective-permute-done | bytes 16416 | tf_op jit(solution)/shard_map/ppermute | solution.py:20
  42.9 5.9 %collective-permute-done.6 = bf16[64,1,128]{2,0,1:T(8,128)(2,1)S(1)} collective-permute-done((bf16[64,1,128]{2,0,1:T(8,128)(2,1)S(1)}, bf16[64,1,128]{2,0,1:T(8,128)(2,1)S(1)}, u32[]{:S(2)}, u32[]{:S(2)}) %collective-permute-start.6) | collective-permute-done | bytes 16416 | tf_op jit(solution)/shard_map/ppermute | solution.py:20
  48.8 5.9 %collective-permute-done.7 = bf16[64,1,128]{2,0,1:T(8,128)(2,1)S(1)} collective-permute-done((bf16[64,1,128]{2,0,1:T(8,128)(2,1)S(1)}, bf16[64,1,128]{2,0,1:T(8,128)(2,1)S(1)}, u32[]{:S(2)}, u32[]{:S(2)}) %collective-permute-start.7) | collective-permute-done | bytes 16416 | tf_op jit(solution)/shard_map/ppermute | solution.py:20
  54.7 5.9 %collective-permute-done.8 = bf16[64,1,128]{2,0,1:T(8,128)(2,1)S(1)} collective-permute-done((bf16[64,1,128]{2,0,1:T(8,128)(2,1)S(1)}, bf16[64,1,128]{2,0,1:T(8,128)(2,1)S(1)}, u32[]{:S(2)}, u32[]{:S(2)}) %collective-permute-start.8) | collective-permute-done | bytes 16416 | tf_op jit(solution)/shard_map/ppermute | solution.py:20
  60.5 5.9 %collective-permute-done.9 = bf16[64,1,128]{2,0,1:T(8,128)(2,1)S(1)} collective-permute-done((bf16[64,1,128]{2,0,1:T(8,128)(2,1)S(1)}, bf16[64,1,128]{2,0,1:T(8,128)(2,1)S(1)}, u32[]{:S(2)}, u32[]{:S(2)}) %collective-permute-start.9) | collective-permute-done | bytes 16416 | tf_op jit(solution)/shard_map/ppermute | solution.py:20
  67.0 5.2 %collective-permute-done.10 = bf16[64,1,128]{2,0,1:T(8,128)(2,1)S(1)} collective-permute-done((bf16[64,1,128]{2,0,1:T(8,128)(2,1)S(1)}, bf16[64,1,128]{2,0,1:T(8,128)(2,1)S(1)}, u32[]{:S(2)}, u32[]{:S(2)}) %collective-permute-start.10) | collective-permute-done | bytes 16416 | tf_op jit(solution)/shard_map/ppermute | solution.py:20
  72.9 5.2 %collective-permute-done.11 = bf16[64,1,128]{2,0,1:T(8,128)(2,1)S(1)} collective-permute-done((bf16[64,1,128]{2,0,1:T(8,128)(2,1)S(1)}, bf16[64,1,128]{2,0,1:T(8,128)(2,1)S(1)}, u32[]{:S(2)}, u32[]{:S(2)}) %collective-permute-start.11) | collective-permute-done | bytes 16416 | tf_op jit(solution)/shard_map/ppermute | solution.py:20
  78.1 5.8 %collective-permute-done.12 = bf16[64,1,128]{2,0,1:T(8,128)(2,1)S(1)} collective-permute-done((bf16[64,1,128]{2,0,1:T(8,128)(2,1)S(1)}, bf16[64,1,128]{2,0,1:T(8,128)(2,1)S(1)}, u32[]{:S(2)}, u32[]{:S(2)}) %collective-permute-start.12) | collective-permute-done | bytes 16416 | tf_op jit(solution)/shard_map/ppermute | solution.py:20
  84.0 5.8 %collective-permute-done.13 = bf16[64,1,128]{2,0,1:T(8,128)(2,1)S(1)} collective-permute-done((bf16[64,1,128]{2,0,1:T(8,128)(2,1)S(1)}, bf16[64,1,128]{2,0,1:T(8,128)(2,1)S(1)}, u32[]{:S(2)}, u32[]{:S(2)}) %collective-permute-start.13) | collective-permute-done | bytes 16416 | tf_op jit(solution)/shard_map/ppermute | solution.py:20
  89.9 5.8 %collective-permute-done.14 = bf16[64,1,128]{2,0,1:T(8,128)(2,1)S(1)} collective-permute-done((bf16[64,1,128]{2,0,1:T(8,128)(2,1)S(1)}, bf16[64,1,128]{2,0,1:T(8,128)(2,1)S(1)}, u32[]{:S(2)}, u32[]{:S(2)}) %collective-permute-start.14) | collective-permute-done | bytes 16416 | tf_op jit(solution)/shard_map/ppermute | solution.py:20
  95.9 0.7 constant_dynamic-update-slice_fusion.16
  96.8 0.7 constant_dynamic-update-slice_fusion
  98.1 5.8 %select_reduce_fusion = (f32[8,8,8]{2,1,0:T(8,128)S(1)}, f32[8,8,8,512]{3,2,1,0:T(8,128)S(1)}) fusion(pred[8,512]{1,0:T(8,128)(4,1)S(1)} %add_compare_fusion, bf16[8,512,8,128]{3,2,1,0:T(8,128)(2,1)} %param.6, bf16[8,8,8,128]{3,2,1,0:T(8,128)(2,1)S(1)} %gather_fusion.1, pred[8]{0:T(512)(128)(4,1)S(1)} %get-tuple-element.8), kind=kOutput, calls=%fused_computation.14 | convolution fusion | flops 67960320 | bytes 9574408 | tf_op jit(solution)/shard_map/vmap(kgd,tkd->kgt)/dot_general | solution.py:8
  104.0 57.6 %pmax.7 = f32[16,8,8]{0,2,1:T(8,128)S(1)} all-reduce(f32[16,8,8]{0,2,1:T(8,128)S(1)} %select_reduce_fusion.1), channel_id=1, replica_groups=mesh['grp'=2,'seq'=16,'head'=1] {'seq'}, use_global_device_ids=true, to_apply=%region_2.3 | all-reduce | flops 1024 | bytes 8192 | tf_op jit(solution)/shard_map/pmax | solution.py:50
  162.8 5.0 %fusion.7 = f32[8,8,8,128]{3,2,1,0:T(8,128)S(1)} fusion(bf16[8,512,8,128]{3,2,1,0:T(8,128)(2,1)} %param.7, f32[8,8,8]{2,1,0:T(8,128)S(1)} %get-tuple-element.6, f32[8,8,8,512]{3,2,1,0:T(8,128)S(1)} %get-tuple-element.13, f32[8,8,8]{2,1,0:T(8,128)S(1)} %get-tuple-element.12, pred[8,512]{1,0:T(8,128)(4,1)S(1)} %add_compare_fusion), kind=kOutput, calls=%fused_computation.9 | convolution fusion | flops 67960832 | bytes 9707520 | tf_op jit(solution)/shard_map/vmap(kgt,tkd->kgd)/dot_general | solution.py:13
  168.3 1.0 copy.26
  171.0 29.6 %all-reduce = f32[1024]{0:T(1024)S(1)} all-reduce(f32[1024]{0:T(1024)S(1)} %reshape.84), channel_id=3, replica_groups=mesh['grp'=2,'seq'=16,'head'=1] {'seq'}, use_global_device_ids=true, to_apply=%region_5.6.clone | all-reduce | flops 1024 | bytes 8192
  200.7 22.7 %reduce-scatter.2.cloned.1.call-done = f32[64,128]{1,0:T(8,128)} async-done(((f32[1024,128]{1,0:T(8,128)}), f32[64,128]{1,0:T(8,128)}) %reduce-scatter.2.cloned.1.call-update) | async-done | bytes 32784 | tf_op jit(solution)/shard_map/reduce_scatter | solution.py:56
  223.4 1.4 fusion.16
  (72 shorter events, 5.8 us)
Async XLA Ops:
  6.5 65.7 %copy-start = (s32[16]{0:T(128)S(1)}, s32[16]{0:T(128)}, u32[]{:S(2)}) copy-start(s32[16]{0:T(128)} %param.8) | copy-start | bytes 196
  6.5 216.9 %reduce-scatter.2.cloned.1.call-start = ((), (), s32[]{:S(2)}) async-start(), calls=%async_computation.1 | async-start | bytes 557056 | tf_op jit(solution)/shard_map/reduce_scatter | solution.py:56
  6.5 7.1 %collective-permute-start = (bf16[64,1,128]{2,0,1:T(8,128)(2,1)}, bf16[64,1,128]{2,0,1:T(8,128)(2,1)S(1)}, u32[]{:S(2)}, u32[]{:S(2)}) collective-permute-start(bf16[64,1,128]{2,0,1:T(8,128)(2,1)} %param.5), channel_id=1, source_target_pairs={{0,1},{1,2},{2,3},{3,4},{4,5},{5,6},{6,7},{7,8},{8,9},{9,10},{10,1... | collective-permute-start | bytes 49160 | tf_op jit(solution)/shard_map/ppermute | solution.py:20
  13.6 5.9 %collective-permute-start.1 = (bf16[64,1,128]{2,0,1:T(8,128)(2,1)S(1)}, bf16[64,1,128]{2,0,1:T(8,128)(2,1)S(1)}, u32[]{:S(2)}, u32[]{:S(2)}) collective-permute-start(bf16[64,1,128]{2,0,1:T(8,128)(2,1)S(1)} %collective-permute-done), channel_id=1, source_target_pairs={{0,1},{1,2},{2,3},{3,4},{4,5},{5,6},{6,7},{7,8},{8,9},{9,10},{10,1... | collective-permute-start | bytes 49160 | tf_op jit(solution)/shard_map/ppermute | solution.py:20
  19.5 5.9 %collective-permute-start.2 = (bf16[64,1,128]{2,0,1:T(8,128)(2,1)S(1)}, bf16[64,1,128]{2,0,1:T(8,128)(2,1)S(1)}, u32[]{:S(2)}, u32[]{:S(2)}) collective-permute-start(bf16[64,1,128]{2,0,1:T(8,128)(2,1)S(1)} %collective-permute-done.1), channel_id=1, source_target_pairs={{0,1},{1,2},{2,3},{3,4},{4,5},{5,6},{6,7},{7,8},{8,9},{9,10},{10,1... | collective-permute-start | bytes 49160 | tf_op jit(solution)/shard_map/ppermute | solution.py:20
  25.3 5.9 %collective-permute-start.3 = (bf16[64,1,128]{2,0,1:T(8,128)(2,1)S(1)}, bf16[64,1,128]{2,0,1:T(8,128)(2,1)S(1)}, u32[]{:S(2)}, u32[]{:S(2)}) collective-permute-start(bf16[64,1,128]{2,0,1:T(8,128)(2,1)S(1)} %collective-permute-done.2), channel_id=1, source_target_pairs={{0,1},{1,2},{2,3},{3,4},{4,5},{5,6},{6,7},{7,8},{8,9},{9,10},{10,1... | collective-permute-start | bytes 49160 | tf_op jit(solution)/shard_map/ppermute | solution.py:20
  31.2 5.9 %collective-permute-start.4 = (bf16[64,1,128]{2,0,1:T(8,128)(2,1)S(1)}, bf16[64,1,128]{2,0,1:T(8,128)(2,1)S(1)}, u32[]{:S(2)}, u32[]{:S(2)}) collective-permute-start(bf16[64,1,128]{2,0,1:T(8,128)(2,1)S(1)} %collective-permute-done.3), channel_id=1, source_target_pairs={{0,1},{1,2},{2,3},{3,4},{4,5},{5,6},{6,7},{7,8},{8,9},{9,10},{10,1... | collective-permute-start | bytes 49160 | tf_op jit(solution)/shard_map/ppermute | solution.py:20
  37.1 5.9 %collective-permute-start.5 = (bf16[64,1,128]{2,0,1:T(8,128)(2,1)S(1)}, bf16[64,1,128]{2,0,1:T(8,128)(2,1)S(1)}, u32[]{:S(2)}, u32[]{:S(2)}) collective-permute-start(bf16[64,1,128]{2,0,1:T(8,128)(2,1)S(1)} %collective-permute-done.4), channel_id=1, source_target_pairs={{0,1},{1,2},{2,3},{3,4},{4,5},{5,6},{6,7},{7,8},{8,9},{9,10},{10,1... | collective-permute-start | bytes 49160 | tf_op jit(solution)/shard_map/ppermute | solution.py:20
  42.9 5.9 %collective-permute-start.6 = (bf16[64,1,128]{2,0,1:T(8,128)(2,1)S(1)}, bf16[64,1,128]{2,0,1:T(8,128)(2,1)S(1)}, u32[]{:S(2)}, u32[]{:S(2)}) collective-permute-start(bf16[64,1,128]{2,0,1:T(8,128)(2,1)S(1)} %collective-permute-done.5), channel_id=1, source_target_pairs={{0,1},{1,2},{2,3},{3,4},{4,5},{5,6},{6,7},{7,8},{8,9},{9,10},{10,1... | collective-permute-start | bytes 49160 | tf_op jit(solution)/shard_map/ppermute | solution.py:20
  48.8 5.9 %collective-permute-start.7 = (bf16[64,1,128]{2,0,1:T(8,128)(2,1)S(1)}, bf16[64,1,128]{2,0,1:T(8,128)(2,1)S(1)}, u32[]{:S(2)}, u32[]{:S(2)}) collective-permute-start(bf16[64,1,128]{2,0,1:T(8,128)(2,1)S(1)} %collective-permute-done.6), channel_id=1, source_target_pairs={{0,1},{1,2},{2,3},{3,4},{4,5},{5,6},{6,7},{7,8},{8,9},{9,10},{10,1... | collective-permute-start | bytes 49160 | tf_op jit(solution)/shard_map/ppermute | solution.py:20
  54.6 5.9 %collective-permute-start.8 = (bf16[64,1,128]{2,0,1:T(8,128)(2,1)S(1)}, bf16[64,1,128]{2,0,1:T(8,128)(2,1)S(1)}, u32[]{:S(2)}, u32[]{:S(2)}) collective-permute-start(bf16[64,1,128]{2,0,1:T(8,128)(2,1)S(1)} %collective-permute-done.7), channel_id=1, source_target_pairs={{0,1},{1,2},{2,3},{3,4},{4,5},{5,6},{6,7},{7,8},{8,9},{9,10},{10,1... | collective-permute-start | bytes 49160 | tf_op jit(solution)/shard_map/ppermute | solution.py:20
  60.5 5.9 %collective-permute-start.9 = (bf16[64,1,128]{2,0,1:T(8,128)(2,1)S(1)}, bf16[64,1,128]{2,0,1:T(8,128)(2,1)S(1)}, u32[]{:S(2)}, u32[]{:S(2)}) collective-permute-start(bf16[64,1,128]{2,0,1:T(8,128)(2,1)S(1)} %collective-permute-done.8), channel_id=1, source_target_pairs={{0,1},{1,2},{2,3},{3,4},{4,5},{5,6},{6,7},{7,8},{8,9},{9,10},{10,1... | collective-permute-start | bytes 49160 | tf_op jit(solution)/shard_map/ppermute | solution.py:20
  66.4 5.9 %collective-permute-start.10 = (bf16[64,1,128]{2,0,1:T(8,128)(2,1)S(1)}, bf16[64,1,128]{2,0,1:T(8,128)(2,1)S(1)}, u32[]{:S(2)}, u32[]{:S(2)}) collective-permute-start(bf16[64,1,128]{2,0,1:T(8,128)(2,1)S(1)} %collective-permute-done.9), channel_id=1, source_target_pairs={{0,1},{1,2},{2,3},{3,4},{4,5},{5,6},{6,7},{7,8},{8,9},{9,10},{10,1... | collective-permute-start | bytes 49160 | tf_op jit(solution)/shard_map/ppermute | solution.py:20
  72.2 5.9 %collective-permute-start.11 = (bf16[64,1,128]{2,0,1:T(8,128)(2,1)S(1)}, bf16[64,1,128]{2,0,1:T(8,128)(2,1)S(1)}, u32[]{:S(2)}, u32[]{:S(2)}) collective-permute-start(bf16[64,1,128]{2,0,1:T(8,128)(2,1)S(1)} %collective-permute-done.10), channel_id=1, source_target_pairs={{0,1},{1,2},{2,3},{3,4},{4,5},{5,6},{6,7},{7,8},{8,9},{9,10},{10,1... | collective-permute-start | bytes 49160 | tf_op jit(solution)/shard_map/ppermute | solution.py:20
  78.1 5.9 %collective-permute-start.12 = (bf16[64,1,128]{2,0,1:T(8,128)(2,1)S(1)}, bf16[64,1,128]{2,0,1:T(8,128)(2,1)S(1)}, u32[]{:S(2)}, u32[]{:S(2)}) collective-permute-start(bf16[64,1,128]{2,0,1:T(8,128)(2,1)S(1)} %collective-permute-done.11), channel_id=1, source_target_pairs={{0,1},{1,2},{2,3},{3,4},{4,5},{5,6},{6,7},{7,8},{8,9},{9,10},{10,1... | collective-permute-start | bytes 49160 | tf_op jit(solution)/shard_map/ppermute | solution.py:20
  84.0 5.9 %collective-permute-start.13 = (bf16[64,1,128]{2,0,1:T(8,128)(2,1)S(1)}, bf16[64,1,128]{2,0,1:T(8,128)(2,1)S(1)}, u32[]{:S(2)}, u32[]{:S(2)}) collective-permute-start(bf16[64,1,128]{2,0,1:T(8,128)(2,1)S(1)} %collective-permute-done.12), channel_id=1, source_target_pairs={{0,1},{1,2},{2,3},{3,4},{4,5},{5,6},{6,7},{7,8},{8,9},{9,10},{10,1... | collective-permute-start | bytes 49160 | tf_op jit(solution)/shard_map/ppermute | solution.py:20
  89.8 5.9 %collective-permute-start.14 = (bf16[64,1,128]{2,0,1:T(8,128)(2,1)S(1)}, bf16[64,1,128]{2,0,1:T(8,128)(2,1)S(1)}, u32[]{:S(2)}, u32[]{:S(2)}) collective-permute-start(bf16[64,1,128]{2,0,1:T(8,128)(2,1)S(1)} %collective-permute-done.13), channel_id=1, source_target_pairs={{0,1},{1,2},{2,3},{3,4},{4,5},{5,6},{6,7},{7,8},{8,9},{9,10},{10,1... | collective-permute-start | bytes 49160 | tf_op jit(solution)/shard_map/ppermute | solution.py:20
  103.9 65.4 %copy-start.1 = (u32[32]{0:T(128)S(1)}, u32[32]{0:T(128)}, u32[]{:S(2)}) copy-start(u32[32]{0:T(128)} %constant.112) | copy-start | bytes 388
Sparse Core Ops, SparseCore 0:
  169.4 53.9 reduce-scatter.1
